TPU v7x, 32 devices: a whole 2x2x4 slice. The times are simulated.
32 devices in a mesh: dp: 4 (over x, core), fsdp: 4 (over z), tp: 2 (over y).
Axes of the slice: x: 2, y: 2, z: 4, core: 2. Of those that a mesh axis runs over, the one named last changes fastest.
Arguments:
- hidden: bfloat16 [8192, 7168], P(('dp', 'fsdp')), may hold values from -6 to 6
- cotangent: bfloat16 [8192, 576], P(('dp', 'fsdp'), 'tp'), may hold values from -6 to 6
- rewards: int32 [64], P(('dp', 'fsdp')), may hold values from 0 to 8
- groups: int32 [64], P(('dp', 'fsdp')), may hold values from 0 to 3, as said below
- lengths: int32 [64], P(('dp', 'fsdp')), may hold values from 1 to 128
- master: float32 [4, 1792, 576], P('fsdp', 'dp', 'tp'), may hold values from -6 to 6
Outputs:
- grad_owned: float32 [4, 1792, 576], P('fsdp', 'dp', 'tp')
- rollout: bfloat16 [4, 1792, 576], P('fsdp')
Inputs may be any that keep to these rules, and one draw needn't show every extreme that they name: `groups`: each prompt number names exactly 16 samples.
All inputs are finite; a program needn't handle non-finite values.
Results may differ from a plain program's by a relative error of at most 0.0033.
Values may be sent and summed in bfloat16 or wider, within the bound.
A program may use at most 64 MiB of HBM per device.

v0:
```python
import jax
import jax.numpy as jnp
from jax import lax
from jax.sharding import PartitionSpec as P

D = 7168
GROUP = 16


def exact_dot(left, right):
    return jnp.dot(left, right, precision=lax.Precision.HIGHEST)


def shards(hidden, cotangent, rewards, groups, lengths, master):
    fsdp_size = lax.axis_size("fsdp")
    dp_size = lax.axis_size("dp")
    samp_local = rewards.shape[0]
    group_count = samp_local * dp_size * fsdp_size // GROUP
    labels = jnp.arange(group_count, dtype=jnp.int32)
    reward_f = rewards.astype(jnp.float32)
    local_onehot = (groups[:, None] == labels[None, :]).astype(jnp.float32)
    totals, squares = lax.psum(
        (exact_dot(reward_f, local_onehot), exact_dot(reward_f * reward_f, local_onehot)),
        ("dp", "fsdp"),
    )
    group_mean = totals / GROUP
    group_square = squares / GROUP
    sample_mean = exact_dot(local_onehot, group_mean)
    sample_square = exact_dot(local_onehot, group_square)
    advantage = (reward_f - sample_mean) / jnp.sqrt(sample_square - sample_mean * sample_mean + 1.0)
    seq_len = hidden.shape[0] // samp_local
    positions = jnp.arange(seq_len, dtype=jnp.int32)
    live = (positions[None, :] < lengths[:, None]).astype(jnp.float32)
    scale = (advantage[:, None] * live / lengths[:, None].astype(jnp.float32)).reshape(
        hidden.shape[0]
    )
    weighted = (cotangent.astype(jnp.float32) * scale[:, None]).astype(jnp.bfloat16)
    cols_local = cotangent.shape[1]
    block_rows = D // fsdp_size
    product = jnp.einsum("td,tc->dc", hidden, weighted, preferred_element_type=jnp.float32)
    reduced = lax.psum_scatter(
        product.reshape(1 * lax.axis_size("fsdp"), block_rows, cols_local),
        "fsdp",
        scatter_dimension=0,
        tiled=True,
    )
    owned = lax.psum_scatter(reduced, "dp", scatter_dimension=1, tiled=True)
    updated = (master - 0.1 * owned).astype(jnp.bfloat16)
    full_rows = lax.all_gather(updated, "tp", axis=2, tiled=True)
    rollout = lax.all_gather(full_rows, "dp", axis=1, tiled=True)
    return (owned, rollout)


def solution(mesh):
    placed = (
        P(("dp", "fsdp"), None),
        P(("dp", "fsdp"), "tp"),
        P(("dp", "fsdp")),
        P(("dp", "fsdp")),
        P(("dp", "fsdp")),
        P("fsdp", "dp", "tp"),
    )
    return jax.shard_map(
        shards,
        mesh=mesh,
        in_specs=placed,
        out_specs=(P("fsdp", "dp", "tp"), P("fsdp", None, None)),
        check_vma=False,
    )
```

profile of v0, /device:TPU:0, one launch (start us, length us, event | category | flops | bytes accessed | tf_op | source)
XLA Modules:
  0.0 288.7 jit_solution(1073819493120630368)
XLA Ops:
  7.2 0.0 reduce-scatter.5.cloned.1.call-start
  7.2 0.9 convolution_bitcast_fusion.1
  8.1 0.9 convolution_bitcast_fusion.3
  8.9 0.7 convert_element_type.20
  9.6 35.1 %all-reduce = (f32[4]{0:T(128)S(1)}, f32[4]{0:T(128)S(1)}) all-reduce(f32[4]{0:T(128)S(1)} %convolution_bitcast_fusion.3, f32[4]{0:T(128)S(1)} %convolution_bitcast_fusion.1), channel_id=1, replica_groups=mesh['dp'=4,'fsdp'=4,'tp'=2] {'dp','fsdp'}, use_global_device_ids=true, to_apply=%region_0.0 | all-reduce | flops 8 | bytes 64 | tf_op jit(solution)/shard_map/psum | solution.py:22
  44.7 0.8 convolution_bitcast_fusion.2
  45.6 0.9 fusion.3
  46.4 0.7 divide_bitcast_fusion
  47.2 5.5 %fusion.4 = f32[288,7168]{1,0:T(8,128)S(1)} fusion(bf16[512,7168]{1,0:T(8,128)(2,1)} %param.6, bf16[512,288]{0,1:T(8,128)(2,1)} %param.7, f32[512]{0:T(512)S(1)} %divide_bitcast_fusion), kind=kOutput, calls=%fused_computation.13 | convolution fusion | flops 2114371584 | bytes 15894528 | tf_op jit(solution)/shard_map/td,tc->dc/dot_general | solution.py:40
  52.7 3.8 %copy.18 = f32[36,4,8,1792]{3,2,0,1:T(8,128)} copy(f32[36,4,8,1792]{3,2,1,0:T(8,128)S(1)} %bitcast.43) | data formatting | bytes 16515072 | tf_op jit(solution)/shard_map/reshape | solution.py:42
  56.5 0.0 reduce-scatter.5.cloned.1.call-update
  56.6 0.0 reduce-scatter.7.cloned.1.call-start
  56.6 139.9 %reduce-scatter.5.cloned.1.call-done = f32[1,1792,288]{1,2,0:T(8,128)} async-done(((f32[4,1792,288]{1,2,0:T(8,128)}), f32[1,1792,288]{1,2,0:T(8,128)}) %reduce-scatter.5.cloned.1.call-update) | async-done | bytes 2064400 | tf_op jit(solution)/shard_map/reduce_scatter | solution.py:41
  196.5 6.9 %copy.12 = f32[1,1792,288]{2,0,1:T(1,128)S(1)} copy(f32[1,1792,288]{1,2,0:T(8,128)} %reduce-scatter.5.cloned.1.call-done) | data formatting | bytes 4128768
  203.4 1.7 copy.19
  205.1 0.0 all-gather.2.cloned.1.call-start
  205.2 36.0 %reduce-scatter.7.cloned.1.call-done = f32[448,288]{1,0:T(8,128)} async-done(((f32[1792,288]{1,0:T(8,128)}), f32[448,288]{1,0:T(8,128)}) %reduce-scatter.7.cloned.1.call-update) | async-done | bytes 516112
  241.2 1.6 reshape_bitcast_fusion
  242.8 1.0 copy.13
  243.8 0.1 subtract_convert_fusion
  243.9 9.2 %all_gather.6 = bf16[1,448,576]{1,2,0:T(8,128)(2,1)S(1)} all-gather(bf16[1,448,288]{1,2,0:T(8,128)(2,1)S(1)} %subtract_convert_fusion), channel_id=1, replica_groups=mesh['dp'=4,'fsdp'=4,'tp'=2] {'tp'}, dimensions={2}, use_global_device_ids=true | all-gather | bytes 774144 | tf_op jit(solution)/shard_map/all_gather | solution.py:49
  253.2 1.1 copy.10
  254.3 23.8 %all-gather.2.cloned.1.call-done = bf16[1,1792,576]{2,1,0:T(8,128)(2,1)} async-done(((bf16[1,448,576]{2,1,0:T(8,128)(2,1)}), bf16[1,1792,576]{2,1,0:T(8,128)(2,1)}) %all-gather.2.cloned.1.call-update) | async-done | bytes 2064400 | tf_op jit(solution)/shard_map/all_gather | solution.py:50
  278.1 4.1 %copy.11 = bf16[1,1792,576]{1,2,0:T(8,128)(2,1)} copy(bf16[1,1792,576]{2,1,0:T(8,128)(2,1)} %all-gather.2.cloned.1.call-done) | data formatting | bytes 4128768
  (6 shorter events, 0.0 us)
Async XLA Ops:
  7.2 189.3 %reduce-scatter.5.cloned.1.call-start = ((), (), s32[]{:S(2)}) async-start(), calls=%async_computation.2 | async-start | bytes 10321920 | tf_op jit(solution)/shard_map/reduce_scatter | solution.py:41
  56.5 187.2 %copy-start.1 = (f32[1,448,288]{1,2,0:T(8,128)S(1)}, f32[1,448,288]{1,2,0:T(8,128)}, u32[]{:S(2)}) copy-start(f32[1,448,288]{1,2,0:T(8,128)} %param.11) | copy-start | bytes 1548292
  56.6 184.6 %reduce-scatter.7.cloned.1.call-start = ((), (), s32[]{:S(2)}) async-start(), calls=%async_computation.4 | async-start | bytes 3440640
  205.1 73.0 %all-gather.2.cloned.1.call-start = ((), (), s32[]{:S(2)}) async-start(), calls=%async_computation.3 | async-start | bytes 2867200 | tf_op jit(solution)/shard_map/all_gather | solution.py:50
  243.8 38.4 %copy-start = (f32[1,448,288]{1,2,0:T(8,128)}, f32[1,448,288]{1,2,0:T(8,128)S(1)}, u32[]{:S(2)}) copy-start(f32[1,448,288]{1,2,0:T(8,128)S(1)} %copy.13) | copy-start | bytes 1548292
Sparse Core Ops, SparseCore 0:
  56.7 139.7 reduce-scatter.4
  205.2 35.8 reduce-scatter.6
  254.4 23.6 all-gather.1
where the time goes:
time: 289 us
  waiting for transfers between devices  200 us (69%)
  blocking collectives  44.4 us (15%)
  local copies, waits for them, and re-layouts  20.2 us (7%)
  between operations  13.8 us (5%)
  matrix products  8.94 us (3%)
    reduce_scatter x1, waiting for transfers between devices, shards(): lax.psum_scatter(product.reshape(1 * lax.axis_size('fsdp'), block_rows, c...  140 us
    unnamed x4, waiting for transfers between devices  36.1 us
    psum x1, blocking collectives, shards(): lax.psum((exact_dot(reward_f, local_onehot), exact_dot(reward_f * reward_...  35.1 us
    all_gather x1, waiting for transfers between devices, shards(): rollout = lax.all_gather(full_rows, 'dp', axis=1, tiled=True)  23.8 us
    unnamed x9, local copies, waits for them, and re-layouts  15.3 us
    all_gather x1, blocking collectives, shards(): full_rows = lax.all_gather(updated, 'tp', axis=2, tiled=True)  9.24 us
  transfers between devices with their start and end apart: 3, of which 3 were waited for; matrix products, arithmetic and copies ran while one was open for 0% of the time, Pallas kernels for 0%

commit v1 on v0

--- a/solution.py
+++ b/solution.py
@@ -47,7 +47,10 @@
     owned = lax.psum_scatter(reduced, "dp", scatter_dimension=1, tiled=True)
     updated = (master - 0.1 * owned).astype(jnp.bfloat16)
     full_rows = lax.all_gather(updated, "tp", axis=2, tiled=True)
-    rollout = lax.all_gather(full_rows, "dp", axis=1, tiled=True)
+    create_node_here = lambda payload, d0: jnp.concatenate(
+        lax.all_gather(payload, axis_name="dp"), axis=d0
+    )
+    rollout = create_node_here(full_rows, 1)
     return (owned, rollout)
 
 

time: 289 us -> 289 us (level)
  no operation moved by 1% of the time
where the time goes in v1:
time: 289 us
  waiting for transfers between devices  200 us (69%)
  blocking collectives  44.4 us (15%)
  local copies, waits for them, and re-layouts  20.2 us (7%)
  between operations  13.8 us (5%)
  matrix products  8.94 us (3%)
    reduce_scatter x1, waiting for transfers between devices, shards(): lax.psum_scatter(product.reshape(1 * lax.axis_size('fsdp'), block_rows, c...  140 us
    unnamed x4, waiting for transfers between devices  36.1 us
    psum x1, blocking collectives, shards(): lax.psum((exact_dot(reward_f, local_onehot), exact_dot(reward_f * reward_...  35.1 us
    all_gather x1, waiting for transfers between devices, shards(): lax.all_gather(payload, axis_name='dp')  23.8 us
    unnamed x9, local copies, waits for them, and re-layouts  15.3 us
    all_gather x1, blocking collectives, shards(): full_rows = lax.all_gather(updated, 'tp', axis=2, tiled=True)  9.24 us
  transfers between devices with their start and end apart: 3, of which 3 were waited for; matrix products, arithmetic and copies ran while one was open for 0% of the time, Pallas kernels for 0%

profile of v1, /device:TPU:0, one launch (start us, length us, event | category | flops | bytes accessed | tf_op | source)
XLA Modules:
  0.0 288.7 jit_solution(1073819493120630368)
XLA Ops:
  7.2 0.0 reduce-scatter.5.cloned.1.call-start
  7.2 0.9 convolution_bitcast_fusion.1
  8.1 0.9 convolution_bitcast_fusion.3
  8.9 0.7 convert_element_type.20
  9.6 35.1 %all-reduce = (f32[4]{0:T(128)S(1)}, f32[4]{0:T(128)S(1)}) all-reduce(f32[4]{0:T(128)S(1)} %convolution_bitcast_fusion.3, f32[4]{0:T(128)S(1)} %convolution_bitcast_fusion.1), channel_id=1, replica_groups=mesh['dp'=4,'fsdp'=4,'tp'=2] {'dp','fsdp'}, use_global_device_ids=true, to_apply=%region_0.0 | all-reduce | flops 8 | bytes 64 | tf_op jit(solution)/shard_map/psum | solution.py:22
  44.7 0.8 convolution_bitcast_fusion.2
  45.6 0.9 fusion.3
  46.4 0.7 divide_bitcast_fusion
  47.2 5.5 %fusion.4 = f32[288,7168]{1,0:T(8,128)S(1)} fusion(bf16[512,7168]{1,0:T(8,128)(2,1)} %param.6, bf16[512,288]{0,1:T(8,128)(2,1)} %param.7, f32[512]{0:T(512)S(1)} %divide_bitcast_fusion), kind=kOutput, calls=%fused_computation.13 | convolution fusion | flops 2114371584 | bytes 15894528 | tf_op jit(solution)/shard_map/td,tc->dc/dot_general | solution.py:40
  52.7 3.8 %copy.22 = f32[36,4,8,1792]{3,2,0,1:T(8,128)} copy(f32[36,4,8,1792]{3,2,1,0:T(8,128)S(1)} %bitcast.44) | data formatting | bytes 16515072 | tf_op jit(solution)/shard_map/reshape | solution.py:42
  56.5 0.0 reduce-scatter.5.cloned.1.call-update
  56.6 0.0 reduce-scatter.7.cloned.1.call-start
  56.6 139.9 %reduce-scatter.5.cloned.1.call-done = f32[1,1792,288]{1,2,0:T(8,128)} async-done(((f32[4,1792,288]{1,2,0:T(8,128)}), f32[1,1792,288]{1,2,0:T(8,128)}) %reduce-scatter.5.cloned.1.call-update) | async-done | bytes 2064400 | tf_op jit(solution)/shard_map/reduce_scatter | solution.py:41
  196.5 6.9 %copy.16 = f32[1,1792,288]{2,0,1:T(1,128)S(1)} copy(f32[1,1792,288]{1,2,0:T(8,128)} %reduce-scatter.5.cloned.1.call-done) | data formatting | bytes 4128768
  203.4 1.7 copy.23
  205.1 0.0 all-gather.3.cloned.1.call-start
  205.2 36.0 %reduce-scatter.7.cloned.1.call-done = f32[448,288]{1,0:T(8,128)} async-done(((f32[1792,288]{1,0:T(8,128)}), f32[448,288]{1,0:T(8,128)}) %reduce-scatter.7.cloned.1.call-update) | async-done | bytes 516112
  241.2 1.6 reshape_bitcast_fusion
  242.8 1.0 copy.17
  243.8 0.1 subtract_convert_fusion
  243.9 9.2 %all_gather.9 = bf16[1,448,576]{1,2,0:T(8,128)(2,1)S(1)} all-gather(bf16[1,448,288]{1,2,0:T(8,128)(2,1)S(1)} %subtract_convert_fusion), channel_id=1, replica_groups=mesh['dp'=4,'fsdp'=4,'tp'=2] {'tp'}, dimensions={2}, use_global_device_ids=true | all-gather | bytes 774144 | tf_op jit(solution)/shard_map/all_gather | solution.py:49
  253.2 1.1 copy.14
  254.3 23.8 %all-gather.3.cloned.1.call-done = bf16[4,448,576]{2,1,0:T(8,128)(2,1)} async-done(((bf16[1,448,576]{2,1,0:T(8,128)(2,1)}), bf16[4,448,576]{2,1,0:T(8,128)(2,1)}) %all-gather.3.cloned.1.call-update) | async-done | bytes 2064400 | tf_op jit(solution)/shard_map/all_gather | solution.py:51
  278.1 4.1 %copy.15 = bf16[1,1792,576]{1,2,0:T(8,128)(2,1)} copy(bf16[1,1792,576]{2,1,0:T(8,128)(2,1)} %bitcast.48) | data formatting | bytes 4128768
  (6 shorter events, 0.0 us)
Async XLA Ops:
  7.2 189.3 %reduce-scatter.5.cloned.1.call-start = ((), (), s32[]{:S(2)}) async-start(), calls=%async_computation.2 | async-start | bytes 10321920 | tf_op jit(solution)/shard_map/reduce_scatter | solution.py:41
  56.5 187.2 %copy-start.1 = (f32[1,448,288]{1,2,0:T(8,128)S(1)}, f32[1,448,288]{1,2,0:T(8,128)}, u32[]{:S(2)}) copy-start(f32[1,448,288]{1,2,0:T(8,128)} %param.11) | copy-start | bytes 1548292
  56.6 184.6 %reduce-scatter.7.cloned.1.call-start = ((), (), s32[]{:S(2)}) async-start(), calls=%async_computation.4 | async-start | bytes 3440640
  205.1 73.0 %all-gather.3.cloned.1.call-start = ((), (), s32[]{:S(2)}) async-start(), calls=%async_computation.3 | async-start | bytes 2867200 | tf_op jit(solution)/shard_map/all_gather | solution.py:51
  243.8 38.4 %copy-start = (f32[1,448,288]{1,2,0:T(8,128)}, f32[1,448,288]{1,2,0:T(8,128)S(1)}, u32[]{:S(2)}) copy-start(f32[1,448,288]{1,2,0:T(8,128)S(1)} %copy.17) | copy-start | bytes 1548292
Sparse Core Ops, SparseCore 0:
  56.7 139.7 reduce-scatter.4
  205.2 35.8 reduce-scatter.6
  254.4 23.6 all-gather.2
